TPU v7x, 32 devices: a whole 2x2x4 slice. The times are simulated.
32 devices in a mesh: dp: 16 (over z, y, x), tensor: 2 (over core).
Axes of the slice: x: 2, y: 2, z: 4, core: 2. Of those that a mesh axis runs over, the one named last changes fastest.
Arguments:
- inputs: bfloat16 [4, 8192, 768], P(None, ('dp', 'tensor')), may hold values from -6 to 6
- lengths: int32 [4, 16], P(None, 'dp'), may hold values from 128 to 512, as said below
- bounds: int32 [4, 16], P(None, 'dp'), may hold values from 32 to 384, as said below
- query_matrix: bfloat16 [768, 768], P('dp', 'tensor'), may hold values from -0.21875 to 0.21875
- key_matrix: bfloat16 [768, 768], P('dp', 'tensor'), may hold values from -0.21875 to 0.21875
- value_matrix: bfloat16 [768, 768], P('dp', 'tensor'), may hold values from -0.21875 to 0.21875
- query_value_bias: float32 [2, 768], P(None, 'tensor'), may hold values from -3 to 3
- adapter_down_weight: bfloat16 [2, 768, 8], P(None, 'dp'), may hold values from -0.21875 to 0.21875
- adapter_up_weight: bfloat16 [2, 8, 768], P(None, None, 'tensor'), may hold values from -1 to 1
- attention_output_weight: bfloat16 [768, 768], P('tensor', 'dp'), may hold values from -1.75 to 1.75
- feedforward_input_weight: bfloat16 [768, 3072], P('dp', 'tensor'), may hold values from -0.21875 to 0.21875
- feedforward_input_bias: float32 [3072], P('tensor'), may hold values from -3 to 3
- feedforward_output_weight: bfloat16 [3072, 768], P('tensor', 'dp'), may hold values from -0.109375 to 0.109375
- output_bias: float32 [2, 768], replicated, may hold values from -3 to 3
- layernorm_scale: float32 [2, 768], replicated, may hold values from 0.5 to 1.5
- layernorm_bias: float32 [2, 768], replicated, may hold values from -2 to 2
- output_gradient: bfloat16 [4, 8192, 768], P(None, ('dp', 'tensor')), may hold values from -6 to 6
Outputs:
- outputs: bfloat16 [4, 8192, 768], P(None, ('dp', 'tensor'))
- input_grad: float32 [4, 8192, 768], P(None, ('dp', 'tensor'))
- lora_up_grad: float32 [2, 8, 768], P(None, None, 'tensor')
Inputs may be any that keep to these rules, and one draw needn't show every extreme that they name: Item i of micro-batch m has live positions 0 to lengths[m, i] - 1 of its 512; the others are padding. An item's first segment is positions 0 to bounds - 1, its second bounds to 511; bounds lies between lengths // 4 and 3 * lengths // 4.
All inputs are finite; a program needn't handle non-finite values.
Results may differ from a plain program's by a relative error of at most 0.015.
The roundings to bfloat16 on the way count: a program that leaves them out, or rounds other values in their place, can miss the bound.
Values may be sent and summed in bfloat16 or wider, within the bound.
No kernel may reach another device: no remote copies, remote signals or barrier semaphores. Data moves between devices by JAX's collectives and lax.ppermute only.
A program may use at most 192 MiB of HBM per device.

v0:
```python
import jax
import jax.numpy as jnp
from jax import lax
from jax.sharding import PartitionSpec as P

HEAD_DIM = 64
UPDATE_RANK = 8
SLOT = 512
adapter_scale = 2.0
masked_value = -1000000000.0
norm_eps = 1e-05
highest_precision = lax.Precision.HIGHEST


def layer_norm(value_rows, gain, shift):
    centre = value_rows - jnp.mean(value_rows, axis=-1, keepdims=True)
    spread = jnp.mean(centre * centre, axis=-1, keepdims=True)
    return centre * lax.rsqrt(spread + norm_eps) * gain + shift


def exact_gelu(value_rows):
    return jax.nn.gelu(value_rows, approximate=False)


def item_mask(length, bound):
    places = jnp.arange(SLOT)
    segment = places >= bound
    return (places < length)[None, :] & (segment[:, None] == segment[None, :])


def split_heads(input_array):
    return input_array.reshape(input_array.shape[0], input_array.shape[1] // HEAD_DIM, HEAD_DIM)


def item_scores(query_heads, key_heads, length, bound):
    scores = (
        jnp.einsum("qhd,khd->hqk", query_heads, key_heads, preferred_element_type=jnp.float32)
        * 0.125
    )
    return jnp.where(item_mask(length, bound)[None], scores, masked_value)


def attend_forward(pieces):
    query_rows, keys, value_rows, length, bound = pieces
    query_heads = split_heads(query_rows)
    value_heads = split_heads(value_rows)
    scores = item_scores(query_heads, split_heads(keys), length, bound)
    peak = jnp.max(scores, axis=-1, keepdims=True)
    totals = jnp.log(jnp.sum(jnp.exp(scores - peak), axis=-1, keepdims=True)) + peak
    soft_weights = jnp.exp(scores - totals).astype(jnp.bfloat16)
    mixed = jnp.einsum(
        "hqk,khd->qhd", soft_weights, value_heads, preferred_element_type=jnp.float32
    )
    return (mixed.reshape(SLOT, query_rows.shape[1]).astype(jnp.bfloat16), totals)


def attend_backward(pieces):
    query_rows, keys, value_rows, grad_mixed, totals, length, bound = pieces
    query_heads = split_heads(query_rows)
    key_heads = split_heads(keys)
    grad_heads = split_heads(grad_mixed)
    scores = item_scores(query_heads, key_heads, length, bound)
    probs = jnp.exp(scores - totals)
    value_gradient = jnp.einsum(
        "hqk,qhd->khd", probs.astype(jnp.bfloat16), grad_heads, preferred_element_type=jnp.float32
    )
    grad_probs = jnp.einsum(
        "qhd,khd->hqk", grad_heads, split_heads(value_rows), preferred_element_type=jnp.float32
    )
    inner = jnp.sum(probs * grad_probs, axis=-1, keepdims=True)
    grad_scores = (probs * (grad_probs - inner)).astype(jnp.bfloat16)
    query_gradient = (
        jnp.einsum("hqk,khd->qhd", grad_scores, key_heads, preferred_element_type=jnp.float32)
        * 0.125
    )
    key_gradient = (
        jnp.einsum("hqk,qhd->khd", grad_scores, query_heads, preferred_element_type=jnp.float32)
        * 0.125
    )
    width = query_rows.shape[1]
    return (
        query_gradient.reshape(SLOT, width).astype(jnp.bfloat16),
        key_gradient.reshape(SLOT, width).astype(jnp.bfloat16),
        value_gradient.reshape(SLOT, width).astype(jnp.bfloat16),
    )


def contract_trailing(left, right):
    return lax.dot_general(
        left, right, (((1,), (1,)), ((), ())), preferred_element_type=jnp.float32
    )


def project_row_batch(
    input_rows,
    query_projected,
    key_projected,
    value_projected,
    down_projected,
    query_value_bias,
    adapter_up_weight,
):
    up_weight_float = adapter_up_weight.astype(jnp.float32)
    lowrank_update = jnp.einsum(
        "td,zdr->ztr", input_rows, down_projected, preferred_element_type=jnp.float32
    )
    query_rows = (
        jnp.dot(input_rows, query_projected, preferred_element_type=jnp.float32)
        + query_value_bias[0]
        + adapter_scale
        * jnp.dot(lowrank_update[0], up_weight_float[0], precision=highest_precision)
    ).astype(jnp.bfloat16)
    keys = jnp.dot(input_rows, key_projected, preferred_element_type=jnp.float32).astype(
        jnp.bfloat16
    )
    value_rows = (
        jnp.dot(input_rows, value_projected, preferred_element_type=jnp.float32)
        + query_value_bias[1]
        + adapter_scale
        * jnp.dot(lowrank_update[1], up_weight_float[1], precision=highest_precision)
    ).astype(jnp.bfloat16)
    return (lowrank_update, query_rows, keys, value_rows)


def adapter_components(lowrank_update, query_gradient, value_gradient):
    first_dims = (((0,), (0,)), ((), ()))
    return adapter_scale * jnp.stack(
        [
            lax.dot_general(
                lowrank_update[0],
                query_gradient.astype(jnp.float32),
                first_dims,
                precision=highest_precision,
            ),
            lax.dot_general(
                lowrank_update[1],
                value_gradient.astype(jnp.float32),
                first_dims,
                precision=highest_precision,
            ),
        ]
    )


def input_terms_all(
    query_gradient,
    key_gradient,
    value_gradient,
    query_projected,
    key_projected,
    value_projected,
    down_projected,
    adapter_up_weight,
):
    query_lowrank_gradient = adapter_scale * contract_trailing(query_gradient, adapter_up_weight[0])
    value_lowrank_gradient = adapter_scale * contract_trailing(value_gradient, adapter_up_weight[1])
    down_float = down_projected.astype(jnp.float32)
    total = contract_trailing(query_gradient, query_projected)
    total = total + contract_trailing(key_gradient, key_projected)
    total = total + contract_trailing(value_gradient, value_projected)
    total = total + lax.dot_general(
        query_lowrank_gradient, down_float[0], (((1,), (1,)), ((), ())), precision=highest_precision
    )
    total = total + lax.dot_general(
        value_lowrank_gradient, down_float[1], (((1,), (1,)), ((), ())), precision=highest_precision
    )
    return total


def forward_pass(rows_local, item_lengths, item_bounds, gathered, parameters):
    (
        query_projected,
        key_projected,
        value_projected,
        down_projected,
        out_full,
        ffn_in_full,
        ffn_out_full,
    ) = gathered
    (
        query_value_bias,
        adapter_up_weight,
        feedforward_input_bias,
        output_bias,
        layernorm_scale,
        layernorm_bias,
    ) = parameters
    group_items = item_lengths.shape[0]
    row_groups = lax.all_gather(rows_local, "tensor", axis=0, tiled=True)
    lowrank_update, query_rows, keys, value_rows = project_row_batch(
        row_groups,
        query_projected,
        key_projected,
        value_projected,
        down_projected,
        query_value_bias,
        adapter_up_weight,
    )
    width = query_rows.shape[1]
    item_shape = (group_items, SLOT, width)
    mixed, totals = lax.map(
        attend_forward,
        (
            query_rows.reshape(item_shape),
            keys.reshape(item_shape),
            value_rows.reshape(item_shape),
            item_lengths,
            item_bounds,
        ),
    )
    mixed_rows = mixed.reshape(group_items * SLOT, width)
    attended = lax.psum_scatter(
        jnp.dot(mixed_rows, out_full, preferred_element_type=jnp.float32),
        "tensor",
        scatter_dimension=0,
        tiled=True,
    )
    hidden_sum = rows_local.astype(jnp.float32) + attended + output_bias[0]
    normed = layer_norm(hidden_sum, layernorm_scale[0], layernorm_bias[0])
    pre_act = (
        jnp.dot(
            lax.all_gather(normed.astype(jnp.bfloat16), "tensor", axis=0, tiled=True),
            ffn_in_full,
            preferred_element_type=jnp.float32,
        )
        + feedforward_input_bias
    )
    activated = exact_gelu(pre_act).astype(jnp.bfloat16)
    ffn_total = (
        normed
        + lax.psum_scatter(
            jnp.dot(activated, ffn_out_full, preferred_element_type=jnp.float32),
            "tensor",
            scatter_dimension=0,
            tiled=True,
        )
        + output_bias[1]
    )
    result = layer_norm(ffn_total, layernorm_scale[1], layernorm_bias[1]).astype(jnp.bfloat16)
    kept = (lowrank_update, query_rows, keys, value_rows, totals, hidden_sum, pre_act, ffn_total)
    return (result, kept)


def layer_backward(grad_out, item_lengths, item_bounds, gathered, parameters, kept):
    (
        query_projected,
        key_projected,
        value_projected,
        down_projected,
        out_full,
        ffn_in_full,
        ffn_out_full,
    ) = gathered
    (
        query_value_bias,
        adapter_up_weight,
        feedforward_input_bias,
        output_bias,
        layernorm_scale,
        layernorm_bias,
    ) = parameters
    lowrank_update, query_rows, keys, value_rows, totals, hidden_sum, pre_act, ffn_total = kept
    group_items = item_lengths.shape[0]
    outer_pull = jax.vjp(
        lambda field: layer_norm(field, layernorm_scale[1], layernorm_bias[1]), ffn_total
    )[1]
    grad_sum = outer_pull(grad_out.astype(jnp.float32))[0]
    grad_act = contract_trailing(
        lax.all_gather(grad_sum.astype(jnp.bfloat16), "tensor", axis=0, tiled=True), ffn_out_full
    )
    gelu_pull = jax.vjp(exact_gelu, pre_act)[1]
    grad_pre = gelu_pull(grad_act)[0].astype(jnp.bfloat16)
    grad_normed = grad_sum + lax.psum_scatter(
        contract_trailing(grad_pre, ffn_in_full), "tensor", scatter_dimension=0, tiled=True
    )
    inner_pull = jax.vjp(
        lambda field: layer_norm(field, layernorm_scale[0], layernorm_bias[0]), hidden_sum
    )[1]
    grad_hidden = inner_pull(grad_normed)[0]
    grad_mixed = contract_trailing(
        lax.all_gather(grad_hidden.astype(jnp.bfloat16), "tensor", axis=0, tiled=True), out_full
    ).astype(jnp.bfloat16)
    width = query_rows.shape[1]
    item_shape = (group_items, SLOT, width)
    query_gradient, key_gradient, value_gradient = lax.map(
        attend_backward,
        (
            query_rows.reshape(item_shape),
            keys.reshape(item_shape),
            value_rows.reshape(item_shape),
            grad_mixed.reshape(item_shape),
            totals,
            item_lengths,
            item_bounds,
        ),
    )
    query_gradient = query_gradient.reshape(group_items * SLOT, width)
    key_gradient = key_gradient.reshape(group_items * SLOT, width)
    value_gradient = value_gradient.reshape(group_items * SLOT, width)
    adapter_portion = adapter_components(lowrank_update, query_gradient, value_gradient)
    row_gradient = grad_hidden + lax.psum_scatter(
        input_terms_all(
            query_gradient,
            key_gradient,
            value_gradient,
            query_projected,
            key_projected,
            value_projected,
            down_projected,
            adapter_up_weight,
        ).astype(jnp.bfloat16),
        "tensor",
        scatter_dimension=0,
        tiled=True,
    ).astype(jnp.float32)
    return (row_gradient, adapter_portion)


def local(
    inputs,
    lengths,
    bounds,
    query_matrix,
    key_matrix,
    value_matrix,
    query_value_bias,
    adapter_down_weight,
    adapter_up_weight,
    attention_output_weight,
    feedforward_input_weight,
    feedforward_input_bias,
    feedforward_output_weight,
    output_bias,
    layernorm_scale,
    layernorm_bias,
    output_gradient,
):
    micro_count = inputs.shape[0]
    parameters = (
        query_value_bias,
        adapter_up_weight,
        feedforward_input_bias,
        output_bias,
        layernorm_scale,
        layernorm_bias,
    )
    result_list = []
    gradient_tree = []
    adapter_combined = jnp.zeros((2, UPDATE_RANK, adapter_up_weight.shape[2]), jnp.float32)
    for batch_index in range(micro_count):
        forward_set = (
            lax.all_gather(query_matrix, "dp", axis=0, tiled=True),
            lax.all_gather(key_matrix, "dp", axis=0, tiled=True),
            lax.all_gather(value_matrix, "dp", axis=0, tiled=True),
            lax.all_gather(adapter_down_weight, "dp", axis=1, tiled=True),
            lax.all_gather(attention_output_weight, "dp", axis=1, tiled=True),
            lax.all_gather(feedforward_input_weight, "dp", axis=0, tiled=True),
            lax.all_gather(feedforward_output_weight, "dp", axis=1, tiled=True),
        )
        result, kept = forward_pass(
            inputs[batch_index], lengths[batch_index], bounds[batch_index], forward_set, parameters
        )
        backward_set = (
            lax.all_gather(query_matrix, "dp", axis=0, tiled=True),
            lax.all_gather(key_matrix, "dp", axis=0, tiled=True),
            lax.all_gather(value_matrix, "dp", axis=0, tiled=True),
            lax.all_gather(adapter_down_weight, "dp", axis=1, tiled=True),
            lax.all_gather(attention_output_weight, "dp", axis=1, tiled=True),
            lax.all_gather(feedforward_input_weight, "dp", axis=0, tiled=True),
            lax.all_gather(feedforward_output_weight, "dp", axis=1, tiled=True),
        )
        row_gradient, adapter_portion = layer_backward(
            output_gradient[batch_index],
            lengths[batch_index],
            bounds[batch_index],
            backward_set,
            parameters,
            kept,
        )
        adapter_combined = adapter_combined + lax.psum(adapter_portion, "dp")
        result_list.append(result)
        gradient_tree.append(row_gradient)
    return (jnp.stack(result_list), jnp.stack(gradient_tree), adapter_combined)


def solution(mesh):
    return jax.shard_map(
        local,
        mesh=mesh,
        in_specs=(
            P(None, ("dp", "tensor"), None),
            P(None, "dp"),
            P(None, "dp"),
            P("dp", "tensor"),
            P("dp", "tensor"),
            P("dp", "tensor"),
            P(None, "tensor"),
            P(None, "dp", None),
            P(None, None, "tensor"),
            P("tensor", "dp"),
            P("dp", "tensor"),
            P("tensor"),
            P("tensor", "dp"),
            P(),
            P(),
            P(),
            P(None, ("dp", "tensor"), None),
        ),
        out_specs=(
            P(None, ("dp", "tensor"), None),
            P(None, ("dp", "tensor"), None),
            P(None, None, "tensor"),
        ),
        check_vma=False,
    )
```

profile of v0, /device:TPU:0, one launch (start us, length us, event | category | flops | bytes accessed | tf_op | source)
XLA Modules:
  0.0 771.6 jit_solution(13941130316083166364)
XLA Ops:
  12.5 44.5 %all_gather.48 = bf16[2,768,8]{2,0,1:T(2,128)(2,1)S(1)} all-gather(bf16[2,48,8]{2,0,1:T(2,128)(2,1)S(1)} %copy.57), channel_id=1, replica_groups=mesh['dp'=16,'tensor'=2] {'dp'}, dimensions={1}, use_global_device_ids=true | all-gather | bytes 26112 | tf_op jit(solution)/shard_map/all_gather | solution.py:355
  57.3 39.2 %all_gather.49 = bf16[768,384]{1,0:T(8,128)(2,1)S(1)} all-gather(bf16[48,384]{1,0:T(8,128)(2,1)} %param.20), channel_id=1, replica_groups=mesh['dp'=16,'tensor'=2] {'dp'}, dimensions={0}, use_global_device_ids=true | all-gather | bytes 626688 | tf_op jit(solution)/shard_map/all_gather | solution.py:352
  96.5 41.1 %all_gather.50 = bf16[768,384]{1,0:T(8,128)(2,1)S(1)} all-gather(bf16[48,384]{1,0:T(8,128)(2,1)} %param.21), channel_id=1, replica_groups=mesh['dp'=16,'tensor'=2] {'dp'}, dimensions={0}, use_global_device_ids=true | all-gather | bytes 626688 | tf_op jit(solution)/shard_map/all_gather | solution.py:353
  137.5 39.3 %all_gather.47 = bf16[768,384]{1,0:T(8,128)(2,1)S(1)} all-gather(bf16[48,384]{1,0:T(8,128)(2,1)} %param.22), channel_id=1, replica_groups=mesh['dp'=16,'tensor'=2] {'dp'}, dimensions={0}, use_global_device_ids=true | all-gather | bytes 626688 | tf_op jit(solution)/shard_map/all_gather | solution.py:354
  176.8 40.8 %all_gather.51 = bf16[384,768]{0,1:T(8,128)(2,1)S(1)} all-gather(bf16[384,48]{0,1:T(8,128)(2,1)} %param.26), channel_id=1, replica_groups=mesh['dp'=16,'tensor'=2] {'dp'}, dimensions={1}, use_global_device_ids=true | all-gather | bytes 626688 | tf_op jit(solution)/shard_map/all_gather | solution.py:356
  218.5 2.4 all-gather.1
  232.9 3.3 all-gather
  247.4 3.1 all-gather.3
  261.4 3.2 all-gather.2
  278.0 2.6 reduce-scatter.25.cloned.1.call-done
  280.6 4.3 fusion.188
  286.7 2.8 all_gather.60
  289.5 47.2 %all-gather.7.cloned.1.call-done = bf16[768,1536]{1,0:T(8,128)(2,1)} async-done(((bf16[48,1536]{1,0:T(8,128)(2,1)}), bf16[768,1536]{1,0:T(8,128)(2,1)}) %all-gather.7.cloned.1.call-update) | async-done | bytes 2359312 | tf_op jit(solution)/shard_map/all_gather | solution.py:357
  336.7 10.4 %fusion.11 = (f32[512,1536]{1,0:T(8,128)}, f32[512,1536]{1,0:T(8,128)}) fusion(f32[1536]{0:T(1024)S(1)} %copy-done.198, bf16[512,768]{1,0:T(8,128)(2,1)S(1)} %all_gather.60, bf16[768,1536]{1,0:T(8,128)(2,1)} %all-gather.7.cloned.1.call-done), kind=kOutput, calls=%fused_computation.39 | convolution fusion | flops 1257504768 | bytes 9443328 | tf_op jit(solution)/shard_map/dot_general | solution.py:221
  347.2 52.7 %all-gather.9.cloned.1.call-done = bf16[1536,768]{0,1:T(8,128)(2,1)} async-done(((bf16[1536,48]{0,1:T(8,128)(2,1)}), bf16[1536,768]{0,1:T(8,128)(2,1)}) %all-gather.9.cloned.1.call-update) | async-done | bytes 2359312 | tf_op jit(solution)/shard_map/all_gather | solution.py:358
  399.9 6.1 fusion.35
  406.1 2.4 all_gather.58
  408.4 9.7 %fusion.10 = (f32[512,1536]{1,0:T(8,128)S(1)}, f32[512,1536]{1,0:T(8,128)S(1)}) fusion(f32[1536]{0:T(1024)} %param.28, bf16[512,768]{1,0:T(8,128)(2,1)S(1)} %all_gather.58, bf16[768,1536]{1,0:T(8,128)(2,1)} %all-gather.7.cloned.1.call-done), kind=kOutput, calls=%fused_computation.38 | convolution fusion | flops 1257504768 | bytes 9443328 | tf_op jit(solution)/shard_map/dot_general | solution.py:221
  420.8 2.7 fusion.34
  423.5 2.4 all_gather.56
  425.9 9.5 %fusion.9 = (f32[512,1536]{1,0:T(8,128)S(1)}, f32[512,1536]{1,0:T(8,128)S(1)}) fusion(f32[1536]{0:T(1024)} %param.28, bf16[512,768]{1,0:T(8,128)(2,1)S(1)} %all_gather.56, bf16[768,1536]{1,0:T(8,128)(2,1)} %all-gather.7.cloned.1.call-done), kind=kOutput, calls=%fused_computation.37 | convolution fusion | flops 1257504768 | bytes 9443328 | tf_op jit(solution)/shard_map/dot_general | solution.py:221
  438.1 2.6 fusion.33
  442.4 5.9 reduce-scatter.23.cloned.1.call-done
  448.4 4.5 fusion.187
  452.9 2.4 all_gather.52
  455.2 8.1 %fusion.8 = (f32[512,1536]{1,0:T(8,128)S(1)}, f32[512,1536]{1,0:T(8,128)S(1)}) fusion(f32[1536]{0:T(1024)S(1)} %copy-done.199, bf16[512,768]{1,0:T(8,128)(2,1)S(1)} %all_gather.52, bf16[768,1536]{1,0:T(8,128)(2,1)S(1)} %copy-done.197), kind=kOutput, calls=%fused_computation.36 | convolution fusion | flops 1257504768 | bytes 9443328 | tf_op jit(solution)/shard_map/dot_general | solution.py:221
  466.0 2.6 fusion.32
  468.7 10.4 %reduce-scatter.19.cloned.1.call-done = f32[256,768]{1,0:T(8,128)} async-done(((f32[512,768]{1,0:T(8,128)}), f32[256,768]{1,0:T(8,128)}) %reduce-scatter.19.cloned.1.call-update) | async-done | bytes 786448 | tf_op jit(solution)/shard_map/reduce_scatter | solution.py:231
  481.0 3.5 fusion.79
  486.7 2.5 all_gather.67
  489.2 7.8 %fusion.43 = f32[512,768]{1,0:T(8,128)} fusion(bf16[768,1536]{1,0:T(8,128)(2,1)} %all-gather.7.cloned.1.call-done, f32[512,1536]{1,0:T(8,128)} %get-tuple-element.339, f32[512,1536]{1,0:T(8,128)} %get-tuple-element.340, bf16[512,768]{1,0:T(8,128)(2,1)} %all_gather.67, bf16[1536,768]{0,1:T(8,128)(2,1)S(1)} %copy-done.4), kind=kOutput, calls=%fused_computation.117 | convolution fusion | flops 2426929152 | bytes 13369344 | tf_op jit(solution)/shard_map/dot_general | solution.py:89
  499.1 4.4 fusion.181
  504.5 2.5 all_gather.65
  507.1 7.8 %fusion.42 = f32[512,768]{1,0:T(8,128)} fusion(bf16[768,1536]{1,0:T(8,128)(2,1)} %all-gather.7.cloned.1.call-done, f32[512,1536]{1,0:T(8,128)} %copy-done.82, f32[512,1536]{1,0:T(8,128)} %copy-done.83, bf16[512,768]{1,0:T(8,128)(2,1)} %all_gather.65, bf16[1536,768]{0,1:T(8,128)(2,1)S(1)} %copy-done.4), kind=kOutput, calls=%fused_computation.116 | convolution fusion | flops 2426929152 | bytes 13369344 | tf_op jit(solution)/shard_map/dot_general | solution.py:89
  516.2 2.9 all_gather.61
  519.1 8.3 %fusion.40 = f32[512,768]{1,0:T(8,128)} fusion(bf16[768,1536]{1,0:T(8,128)(2,1)} %all-gather.7.cloned.1.call-done, f32[512,1536]{1,0:T(8,128)} %copy-done.84, f32[512,1536]{1,0:T(8,128)} %copy-done.85, bf16[512,768]{1,0:T(8,128)(2,1)} %all_gather.61, bf16[1536,768]{0,1:T(8,128)(2,1)S(1)} %copy-done.4), kind=kOutput, calls=%fused_computation.114 | convolution fusion | flops 2426929152 | bytes 13369344 | tf_op jit(solution)/shard_map/dot_general | solution.py:89
  528.8 2.5 all_gather.63
  531.3 7.8 %fusion.41 = f32[512,768]{1,0:T(8,128)} fusion(bf16[768,1536]{1,0:T(8,128)(2,1)} %all-gather.7.cloned.1.call-done, f32[512,1536]{1,0:T(8,128)} %copy-done.80, f32[512,1536]{1,0:T(8,128)} %copy-done.81, bf16[512,768]{1,0:T(8,128)(2,1)} %all_gather.63, bf16[1536,768]{0,1:T(8,128)(2,1)S(1)} %copy-done.4), kind=kOutput, calls=%fused_computation.115 | convolution fusion | flops 2426929152 | bytes 13369344 | tf_op jit(solution)/shard_map/dot_general | solution.py:89
  539.2 2.7 pad_maximum_fusion.1
  542.1 3.1 multiply_reduce_fusion.7
  545.2 5.8 reduce-scatter.37.cloned.1.call-done
  551.0 2.5 fusion.179
  553.7 2.5 all_gather.62
  556.9 4.6 convolution_convert_fusion.6
  564.5 2.5 all_gather.64
  572.1 2.4 all_gather.66
  580.7 2.5 all_gather.68
  588.9 4.6 multiply_reduce_fusion.3
  593.6 6.5 multiply_convert_fusion.3
  603.3 4.8 multiply_reduce_fusion.2
  608.2 4.7 multiply_reduce_fusion.1
  612.8 5.6 multiply_reduce_fusion
  622.1 6.7 multiply_convert_fusion.2
  630.5 4.9 multiply_convert_fusion.1
  637.3 4.7 multiply_convert_fusion
  647.8 2.1 add_convert_fusion.6
  650.3 2.2 convolution_bitcast_fusion.6
  657.6 2.1 add_convert_fusion.5
  659.8 2.1 convolution_bitcast_fusion.8
  667.1 2.1 add_convert_fusion.4
  676.5 77.1 %psum.34 = f32[2,8,384]{2,1,0:T(8,128)} all-reduce(f32[2,8,384]{2,1,0:T(8,128)S(1)} %fusion.110), channel_id=1, replica_groups=mesh['dp'=16,'tensor'=2] {'dp'}, use_global_device_ids=true, to_apply=%region_60.61 | all-reduce | flops 6144 | bytes 49152 | tf_op jit(solution)/shard_map/psum | solution.py:380
  755.6 2.1 add_bitcast_fusion.2
  757.7 2.1 add_bitcast_fusion.1
  761.0 3.1 pad_maximum_fusion
  (638 shorter events, 130.8 us)
Async XLA Ops:
  8.0 270.0 %reduce-scatter.21.cloned.1.call-start = ((), (), s32[]{:S(2)}) async-start(), calls=%async_computation.20 | async-start | bytes 2359296 | tf_op jit(solution)/shard_map/reduce_scatter | solution.py:212
  57.3 207.3 %copy-start.88 = (bf16[2,768,8]{1,2,0:T(8,128)(2,1)}, bf16[2,768,8]{1,2,0:T(8,128)(2,1)S(1)}, u32[]{:S(2)}) copy-start(bf16[2,768,8]{1,2,0:T(8,128)(2,1)S(1)} %copy.58) | copy-start | bytes 73732
  57.3 160.3 %copy-start.53 = (bf16[4,256,768]{2,1,0:T(8,128)(2,1)S(1)}, bf16[4,256,768]{2,1,0:T(8,128)(2,1)}, u32[]{:S(2)}) copy-start(bf16[4,256,768]{2,1,0:T(8,128)(2,1)} %param.17) | copy-start | bytes 4718596
  96.5 168.4 %copy-start.19 = (bf16[768,384]{1,0:T(8,128)(2,1)}, bf16[768,384]{1,0:T(8,128)(2,1)S(1)}, u32[]{:S(2)}) copy-start(bf16[768,384]{1,0:T(8,128)(2,1)S(1)} %all_gather.49) | copy-start | bytes 1769476
  137.5 129.9 %copy-start.14 = (bf16[768,384]{1,0:T(8,128)(2,1)}, bf16[768,384]{1,0:T(8,128)(2,1)S(1)}, u32[]{:S(2)}) copy-start(bf16[768,384]{1,0:T(8,128)(2,1)S(1)} %all_gather.50) | copy-start | bytes 1769476
  176.8 93.8 %copy-start.22 = (bf16[768,384]{1,0:T(8,128)(2,1)}, bf16[768,384]{1,0:T(8,128)(2,1)S(1)}, u32[]{:S(2)}) copy-start(bf16[768,384]{1,0:T(8,128)(2,1)S(1)} %all_gather.47) | copy-start | bytes 1769476
  217.6 56.1 %copy-start.24 = (bf16[384,768]{0,1:T(8,128)(2,1)}, bf16[384,768]{0,1:T(8,128)(2,1)S(1)}, u32[]{:S(2)}) copy-start(bf16[384,768]{0,1:T(8,128)(2,1)S(1)} %all_gather.51) | copy-start | bytes 1769476
  232.9 45.1 %reduce-scatter.17.cloned.1.call-start = ((), (), s32[]{:S(2)}) async-start(), calls=%async_computation.16 | async-start | bytes 2359296 | tf_op jit(solution)/shard_map/reduce_scatter | solution.py:212
  247.3 30.7 %reduce-scatter.29.cloned.1.call-start = ((), (), s32[]{:S(2)}) async-start(), calls=%async_computation.24 | async-start | bytes 2359296 | tf_op jit(solution)/shard_map/reduce_scatter | solution.py:212
  261.3 19.3 %reduce-scatter.25.cloned.1.call-start = ((), (), s32[]{:S(2)}) async-start(), calls=%async_computation.22 | async-start | bytes 2359296 | tf_op jit(solution)/shard_map/reduce_scatter | solution.py:212
  275.5 61.2 %all-gather.7.cloned.1.call-start = ((), (), s32[]{:S(2)}) async-start(), calls=%async_computation.17 | async-start | bytes 2506752 | tf_op jit(solution)/shard_map/all_gather | solution.py:357
  276.1 123.8 %all-gather.9.cloned.1.call-start = ((), (), s32[]{:S(2)}) async-start(), calls=%async_computation.18 | async-start | bytes 2506752 | tf_op jit(solution)/shard_map/all_gather | solution.py:358
  276.7 165.7 %reduce-scatter.31.cloned.1.call-start = ((), (), s32[]{:S(2)}) async-start(), calls=%async_computation.25 | async-start | bytes 2359296 | tf_op jit(solution)/shard_map/reduce_scatter | solution.py:231
  285.1 51.6 %copy-start.198 = (f32[1536]{0:T(1024)S(1)}, f32[1536]{0:T(1024)}, u32[]{:S(2)}) copy-start(f32[1536]{0:T(1024)} %param.28) | copy-start | bytes 18436
  406.0 36.4 %reduce-scatter.27.cloned.1.call-start = ((), (), s32[]{:S(2)}) async-start(), calls=%async_computation.23 | async-start | bytes 2359296 | tf_op jit(solution)/shard_map/reduce_scatter | solution.py:231
  408.4 12.3 %copy-start.4 = (bf16[1536,768]{0,1:T(8,128)(2,1)S(1)}, bf16[1536,768]{0,1:T(8,128)(2,1)}, u32[]{:S(2)}) copy-start(bf16[1536,768]{0,1:T(8,128)(2,1)} %all-gather.9.cloned.1.call-done) | copy-start | bytes 7077892
  423.4 24.9 %reduce-scatter.23.cloned.1.call-start = ((), (), s32[]{:S(2)}) async-start(), calls=%async_computation.21 | async-start | bytes 2359296 | tf_op jit(solution)/shard_map/reduce_scatter | solution.py:231
  438.1 10.2 %copy-start.142 = (f32[768]{0:T(1024)S(1)}, f32[768]{0:T(1024)}, u32[]{:S(2)}) copy-start(f32[768]{0:T(1024)} %get-tuple-element.175) | copy-start | bytes 9220
  438.1 10.2 %copy-start.144 = (f32[256]{0:T(256)S(1)}, f32[256]{0:T(256)}, u32[]{:S(2)}) copy-start(f32[256]{0:T(256)} %copy-done.143) | copy-start | bytes 3076
  438.1 10.2 %copy-start.148 = (f32[256]{0:T(256)S(1)}, f32[256]{0:T(256)}, u32[]{:S(2)}) copy-start(f32[256]{0:T(256)} %copy-done.147) | copy-start | bytes 3076
  438.1 10.2 %copy-start.152 = (f32[256]{0:T(256)S(1)}, f32[256]{0:T(256)}, u32[]{:S(2)}) copy-start(f32[256]{0:T(256)} %copy-done.151) | copy-start | bytes 3076
  438.1 10.2 %copy-start.165 = (f32[256]{0:T(256)S(1)}, f32[256]{0:T(256)}, u32[]{:S(2)}) copy-start(f32[256]{0:T(256)} %copy-done.164) | copy-start | bytes 3076
  438.1 10.2 %copy-start.168 = (f32[256]{0:T(256)S(1)}, f32[256]{0:T(256)}, u32[]{:S(2)}) copy-start(f32[256]{0:T(256)} %copy-done.167) | copy-start | bytes 3076
  438.1 10.2 %copy-start.171 = (f32[256]{0:T(256)S(1)}, f32[256]{0:T(256)}, u32[]{:S(2)}) copy-start(f32[256]{0:T(256)} %copy-done.170) | copy-start | bytes 3076
  440.7 38.3 %reduce-scatter.19.cloned.1.call-start = ((), (), s32[]{:S(2)}) async-start(), calls=%async_computation.19 | async-start | bytes 2359296 | tf_op jit(solution)/shard_map/reduce_scatter | solution.py:231
  442.3 10.6 %copy-start.189 = (f32[256]{0:T(256)}, f32[256]{0:T(256)S(1)}, u32[]{:S(2)}) copy-start(f32[256]{0:T(256)S(1)} %multiply_reduce_fusion.15) | copy-start | bytes 3076
  442.4 36.7 %copy-start.154 = (f32[256]{0:T(256)}, f32[256]{0:T(256)S(1)}, u32[]{:S(2)}) copy-start(f32[256]{0:T(256)S(1)} %fusion.147) | copy-start | bytes 3076
  448.4 6.9 copy-start.197
  448.4 6.9 copy-start.199
  468.6 73.4 %reduce-scatter.45.cloned.1.call-start = ((), (), s32[]{:S(2)}) async-start(), calls=%async_computation.32 | async-start | bytes 2359296 | tf_op jit(solution)/shard_map/reduce_scatter | solution.py:273
  468.6 15.8 %copy-start.179 = (f32[256]{0:T(256)}, f32[256]{0:T(256)S(1)}, u32[]{:S(2)}) copy-start(f32[256]{0:T(256)S(1)} %broadcast_multiply_fusion.4) | copy-start | bytes 3076
  468.6 15.8 %copy-start.180 = (f32[256]{0:T(256)}, f32[256]{0:T(256)S(1)}, u32[]{:S(2)}) copy-start(f32[256]{0:T(256)S(1)} %broadcast_multiply_fusion.2) | copy-start | bytes 3076
  468.7 15.8 %copy-start.182 = (f32[256]{0:T(256)}, f32[256]{0:T(256)S(1)}, u32[]{:S(2)}) copy-start(f32[256]{0:T(256)S(1)} %broadcast_multiply_fusion) | copy-start | bytes 3076
  489.2 10.0 %copy-start.141 = (f32[768]{0:T(1024)S(1)}, f32[768]{0:T(1024)}, u32[]{:S(2)}) copy-start(f32[768]{0:T(1024)} %get-tuple-element.173) | copy-start | bytes 9220
  497.0 45.0 %reduce-scatter.41.cloned.1.call-start = ((), (), s32[]{:S(2)}) async-start(), calls=%async_computation.30 | async-start | bytes 2359296 | tf_op jit(solution)/shard_map/reduce_scatter | solution.py:273
  503.5 11.4 %copy-start.158 = (f32[256]{0:T(256)}, f32[256]{0:T(256)S(1)}, u32[]{:S(2)}) copy-start(f32[256]{0:T(256)S(1)} %negate_multiply_fusion.7) | copy-start | bytes 3076
  507.1 7.9 %copy-start.196 = (f32[256]{0:T(256)S(1)}, f32[256]{0:T(256)}, u32[]{:S(2)}) copy-start(f32[256]{0:T(256)} %get-tuple-element.260) | copy-start | bytes 3076
  514.9 27.1 %reduce-scatter.33.cloned.1.call-start = ((), (), s32[]{:S(2)}) async-start(), calls=%async_computation.26 | async-start | bytes 2359296 | tf_op jit(solution)/shard_map/reduce_scatter | solution.py:273
  515.0 12.5 %copy-start.162 = (f32[256]{0:T(256)}, f32[256]{0:T(256)S(1)}, u32[]{:S(2)}) copy-start(f32[256]{0:T(256)S(1)} %negate_multiply_fusion.11) | copy-start | bytes 3076
  519.1 8.4 %copy-start.195 = (f32[256]{0:T(256)S(1)}, f32[256]{0:T(256)}, u32[]{:S(2)}) copy-start(f32[256]{0:T(256)} %get-tuple-element.194) | copy-start | bytes 3076
  527.5 23.6 %reduce-scatter.37.cloned.1.call-start = ((), (), s32[]{:S(2)}) async-start(), calls=%async_computation.28 | async-start | bytes 2359296 | tf_op jit(solution)/shard_map/reduce_scatter | solution.py:273
  539.1 214.4 %reduce-scatter.35.cloned.1.call-start = ((), (), s32[]{:S(2)}) async-start(), calls=%async_computation.27 | async-start | bytes 1179648 | tf_op jit(solution)/shard_map/reduce_scatter | solution.py:301
  541.9 9.1 %copy-start.153 = (f32[256]{0:T(256)S(1)}, f32[256]{0:T(256)}, u32[]{:S(2)}) copy-start(f32[256]{0:T(256)} %copy-done.151) | copy-start | bytes 3076
  541.9 9.1 %copy-start.155 = (f32[256]{0:T(256)S(1)}, f32[256]{0:T(256)}, u32[]{:S(2)}) copy-start(f32[256]{0:T(256)} %copy-done.154) | copy-start | bytes 3076
  541.9 9.1 %copy-start.161 = (f32[256]{0:T(256)S(1)}, f32[256]{0:T(256)}, u32[]{:S(2)}) copy-start(f32[256]{0:T(256)} %copy-done.160) | copy-start | bytes 3076
  541.9 9.1 %copy-start.163 = (f32[256]{0:T(256)S(1)}, f32[256]{0:T(256)}, u32[]{:S(2)}) copy-start(f32[256]{0:T(256)} %copy-done.162) | copy-start | bytes 3076
  556.9 10.7 %slice-start = ((s8[6291456]{0:T(1024)(128)(4,1)}), s8[4194304]{0:T(1024)(128)(4,1)S(1)}, s32[]{:S(2)}) async-start(s8[6291456]{0:T(1024)(128)(4,1)} %bitcast.410), calls=%async_computation.34 | async-start | bytes 8388608
  564.3 7.7 copy-start.34
  567.5 8.2 %slice-start.8 = ((s8[6291456]{0:T(1024)(128)(4,1)}), s8[4194304]{0:T(1024)(128)(4,1)S(1)}, s32[]{:S(2)}) async-start(s8[6291456]{0:T(1024)(128)(4,1)} %bitcast.418), calls=%async_computation.42 | async-start | bytes 8388608
  567.6 8.2 %slice-start.9 = ((s8[6291456]{0:T(1024)(128)(4,1)}), s8[2097152]{0:T(1024)(128)(4,1)S(1)}, s32[]{:S(2)}) async-start(s8[6291456]{0:T(1024)(128)(4,1)} %bitcast.418), calls=%async_computation.43 | async-start | bytes 4194304
  575.8 8.7 %slice-start.2 = ((s8[6291456]{0:T(1024)(128)(4,1)}), s8[4194304]{0:T(1024)(128)(4,1)S(1)}, s32[]{:S(2)}) async-start(s8[6291456]{0:T(1024)(128)(4,1)} %bitcast.412), calls=%async_computation.36 | async-start | bytes 8388608
  586.4 7.2 copy-start.75
  622.1 133.6 %reduce-scatter.39.cloned.1.call-start = ((), (), s32[]{:S(2)}) async-start(), calls=%async_computation.29 | async-start | bytes 1179648 | tf_op jit(solution)/shard_map/reduce_scatter | solution.py:301
  622.1 8.4 %slice-start.12 = ((s8[6291456]{0:T(1024)(128)(4,1)}), s8[4194304]{0:T(1024)(128)(4,1)S(1)}, s32[]{:S(2)}) async-start(s8[6291456]{0:T(1024)(128)(4,1)} %bitcast.422), calls=%async_computation.46 | async-start | bytes 8388608
  622.1 8.4 %slice-start.13 = ((s8[6291456]{0:T(1024)(128)(4,1)}), s8[2097152]{0:T(1024)(128)(4,1)S(1)}, s32[]{:S(2)}) async-start(s8[6291456]{0:T(1024)(128)(4,1)} %bitcast.422), calls=%async_computation.47 | async-start | bytes 4194304
  649.9 107.8 %reduce-scatter.43.cloned.1.call-start = ((), (), s32[]{:S(2)}) async-start(), calls=%async_computation.31 | async-start | bytes 1179648 | tf_op jit(solution)/shard_map/reduce_scatter | solution.py:301
  659.8 100.1 %reduce-scatter.47.cloned.1.call-start = ((), (), s32[]{:S(2)}) async-start(), calls=%async_computation.33 | async-start | bytes 1179648 | tf_op jit(solution)/shard_map/reduce_scatter | solution.py:301
  667.1 8.6 %copy-start.139 = (f32[1,8,384]{2,1,0:T(8,128)S(1)}, f32[1,8,384]{2,1,0:T(8,128)}, u32[]{:S(2)}) copy-start(f32[1,8,384]{2,1,0:T(8,128)} %convolution_bitcast_fusion.4) | copy-start | bytes 36868
  667.1 86.5 %copy-start.174 = (f32[256]{0:T(256)S(1)}, f32[256]{0:T(256)}, u32[]{:S(2)}) copy-start(f32[256]{0:T(256)} %copy-done.173) | copy-start | bytes 3076
  669.2 84.4 %copy-start.33 = (f32[256,768]{1,0:T(8,128)S(1)}, f32[256,768]{1,0:T(8,128)}, u32[]{:S(2)}) copy-start(f32[256,768]{1,0:T(8,128)} %copy-done.32) | copy-start | bytes 2359300
  669.2 86.4 %copy-start.37 = (f32[256,768]{1,0:T(8,128)S(1)}, f32[256,768]{1,0:T(8,128)}, u32[]{:S(2)}) copy-start(f32[256,768]{1,0:T(8,128)} %copy-done.36) | copy-start | bytes 2359300
  669.2 88.5 %copy-start.35 = (f32[256,768]{1,0:T(8,128)S(1)}, f32[256,768]{1,0:T(8,128)}, u32[]{:S(2)}) copy-start(f32[256,768]{1,0:T(8,128)} %copy-done.34) | copy-start | bytes 2359300
  674.2 85.6 %copy-start.40 = (f32[256,768]{1,0:T(8,128)S(1)}, f32[256,768]{1,0:T(8,128)}, u32[]{:S(2)}) copy-start(f32[256,768]{1,0:T(8,128)} %copy-done.39) | copy-start | bytes 2359300
  674.2 85.6 %copy-start.178 = (f32[256]{0:T(256)S(1)}, f32[256]{0:T(256)}, u32[]{:S(2)}) copy-start(f32[256]{0:T(256)} %copy-done.177) | copy-start | bytes 3076
  (168 other events, 570.6 us)
Sparse Core Ops, SparseCore 0:
  233.0 5.0 reduce-scatter.20
  247.4 5.1 reduce-scatter.16
  261.5 5.1 reduce-scatter.28
  275.6 4.9 reduce-scatter.24
  406.1 7.4 reduce-scatter.30
  423.6 7.4 reduce-scatter.26
  440.8 7.4 reduce-scatter.22
  468.7 10.3 reduce-scatter.18
  497.1 10.3 reduce-scatter.44
  515.0 10.3 reduce-scatter.40
  528.2 10.3 reduce-scatter.32
  540.7 10.3 reduce-scatter.36
  622.2 9.4 reduce-scatter.34
  650.1 9.4 reduce-scatter.38
  661.6 9.2 reduce-scatter.42
  673.6 9.2 reduce-scatter.46
Sparse Core Ops, SparseCore 1:
  278.8 57.9 all-gather.6
  339.4 60.4 all-gather.8
where the time goes:
time: 779 us; the launch traced here: 772 us
  blocking collectives  324 us (42%)
  matrix products  197 us (25%)
  waiting for transfers between devices  126 us (16%)
  other arithmetic  82.3 us (11%)
  local copies, waits for them, and re-layouts  22 us (3%)
  between operations  18.9 us (2%)
    psum x1, blocking collectives, local(): adapter_combined = adapter_combined + lax.psum(adapter_portion, 'dp')  77.1 us
    dot_general x28, matrix products, contract_trailing(): lax.dot_general(left, right, (((1,), (1,)), ((), ())), preferred_element_...  53.7 us
    all_gather x1, waiting for transfers between devices, local(): lax.all_gather(feedforward_output_weight, 'dp', axis=1, tiled=True)  52.7 us
    all_gather x1, waiting for transfers between devices, local(): lax.all_gather(feedforward_input_weight, 'dp', axis=0, tiled=True)  47.2 us
    all_gather x1, blocking collectives, local(): lax.all_gather(adapter_down_weight, 'dp', axis=1, tiled=True)  44.5 us
    all_gather x1, blocking collectives, local(): lax.all_gather(key_matrix, 'dp', axis=0, tiled=True)  41.1 us
    all_gather x1, blocking collectives, local(): lax.all_gather(attention_output_weight, 'dp', axis=1, tiled=True)  40.8 us
    all_gather x1, blocking collectives, local(): lax.all_gather(value_matrix, 'dp', axis=0, tiled=True)  39.3 us
  transfers between devices with their start and end apart: 18, of which 6 were waited for; matrix products, arithmetic and copies ran while one was open for 22% of the time, Pallas kernels for 0%

commit v1 on v0

--- a/solution.py
+++ b/solution.py
@@ -2,6 +2,7 @@
 import jax.numpy as jnp
 from jax import lax
 from jax.sharding import PartitionSpec as P
+from jax.lax import axis_index, axis_size, ppermute
 
 HEAD_DIM = 64
 UPDATE_RANK = 8
@@ -10,6 +11,34 @@
 masked_value = -1000000000.0
 norm_eps = 1e-05
 highest_precision = lax.Precision.HIGHEST
+
+
+def measure_results(block_here, dimension_no):
+    finding = list(block_here.shape[1:])
+    finding[dimension_no] *= block_here.shape[0]
+    b_next = jnp.moveaxis(block_here, 0, dimension_no).reshape(finding)
+    return b_next
+
+
+def notes_meet(shard_in, axis_name):
+    parts_n = axis_size(axis_name)
+    g_now = shard_in[None]
+    for d in range(parts_n.bit_length() - 1):
+        field_out = 1 << d
+        copies = []
+        for k0 in range(parts_n):
+            copies.append((k0, k0 ^ field_out))
+        tall = ppermute(g_now, axis_name, copies)
+        res = jnp.stack([g_now, tall], axis=0)
+        latest = axis_index(axis_name) >> d & 1
+        g_now = jnp.where(latest == 0, res, res[::-1]).reshape(-1, *shard_in.shape)
+    return g_now
+
+
+def _return_all_steps_all(mat, x_part, out_dim):
+    s_next = notes_meet(mat, x_part)
+    y2 = measure_results(s_next, out_dim)
+    return y2
 
 
 def layer_norm(value_rows, gain, shift):
@@ -352,7 +381,7 @@
             lax.all_gather(query_matrix, "dp", axis=0, tiled=True),
             lax.all_gather(key_matrix, "dp", axis=0, tiled=True),
             lax.all_gather(value_matrix, "dp", axis=0, tiled=True),
-            lax.all_gather(adapter_down_weight, "dp", axis=1, tiled=True),
+            _return_all_steps_all(adapter_down_weight, x_part="dp", out_dim=1),
             lax.all_gather(attention_output_weight, "dp", axis=1, tiled=True),
             lax.all_gather(feedforward_input_weight, "dp", axis=0, tiled=True),
             lax.all_gather(feedforward_output_weight, "dp", axis=1, tiled=True),

time: 779 us -> 805 us (1.033)
  matrix products: 197 us -> 211 us
    ppermute x0 -> x4, waiting for transfers between devices: none -> 9.39 us  [notes_meet(): tall = ppermute(g_now, axis_name, copies)]
    unnamed x429 -> x449, local copies, waits for them, and re-layouts: 15.9 us -> 21.8 us
  transfers between devices with their start and end apart: 18 -> 22, of which waited for: 6 -> 8; matrix products, arithmetic and copies ran while one was open for 22% -> 25% of each run, Pallas kernels for 0% -> 0%
where the time goes in v1:
time: 805 us; the launch traced here: 795 us
  blocking collectives  318 us (40%)
  matrix products  211 us (26%)
  waiting for transfers between devices  132 us (16%)
  other arithmetic  81.9 us (10%)
  local copies, waits for them, and re-layouts  28.4 us (4%)
  between operations  19.1 us (2%)
    psum x1, blocking collectives, local(): adapter_combined = adapter_combined + lax.psum(adapter_portion, 'dp')  71.8 us
    dot_general x28, matrix products, contract_trailing(): lax.dot_general(left, right, (((1,), (1,)), ((), ())), preferred_element_...  53.7 us
    all_gather x1, waiting for transfers between devices, local(): lax.all_gather(feedforward_output_weight, 'dp', axis=1, tiled=True)  52.7 us
    all_gather x1, blocking collectives, local(): lax.all_gather(query_matrix, 'dp', axis=0, tiled=True)  43.7 us
    all_gather x1, blocking collectives, local(): lax.all_gather(adapter_down_weight, 'dp', axis=1, tiled=True)  43.4 us
    all_gather x1, waiting for transfers between devices, local(): lax.all_gather(feedforward_input_weight, 'dp', axis=0, tiled=True)  42.1 us
    all_gather x1, blocking collectives, local(): lax.all_gather(value_matrix, 'dp', axis=0, tiled=True)  41.2 us
    all_gather x1, blocking collectives, local(): lax.all_gather(key_matrix, 'dp', axis=0, tiled=True)  38.9 us
  transfers between devices with their start and end apart: 22, of which 8 were waited for; matrix products, arithmetic and copies ran while one was open for 25% of the time, Pallas kernels for 0%

profile of v1, /device:TPU:0, one launch (start us, length us, event | category | flops | bytes accessed | tf_op | source)
XLA Modules:
  0.0 795.1 jit_solution(6737066262286172848)
XLA Ops:
  8.0 3.0 collective-permute-start
  11.9 43.7 %all_gather.48 = bf16[768,384]{1,0:T(8,128)(2,1)S(1)} all-gather(bf16[48,384]{1,0:T(8,128)(2,1)} %param.20), channel_id=1, replica_groups=mesh['dp'=16,'tensor'=2] {'dp'}, dimensions={0}, use_global_device_ids=true | all-gather | bytes 626688 | tf_op jit(solution)/shard_map/all_gather | solution.py:381
  55.6 38.9 %all_gather.49 = bf16[768,384]{1,0:T(8,128)(2,1)S(1)} all-gather(bf16[48,384]{1,0:T(8,128)(2,1)} %param.21), channel_id=1, replica_groups=mesh['dp'=16,'tensor'=2] {'dp'}, dimensions={0}, use_global_device_ids=true | all-gather | bytes 626688 | tf_op jit(solution)/shard_map/all_gather | solution.py:382
  96.2 2.4 all-gather.3
  98.5 2.4 all-gather.2
  105.6 2.4 all-gather
  110.6 2.5 all-gather.1
  116.5 41.2 %all_gather.47 = bf16[768,384]{1,0:T(8,128)(2,1)S(1)} all-gather(bf16[48,384]{1,0:T(8,128)(2,1)S(1)} %copy-done.147), channel_id=1, replica_groups=mesh['dp'=16,'tensor'=2] {'dp'}, dimensions={0}, use_global_device_ids=true | all-gather | bytes 626688 | tf_op jit(solution)/shard_map/all_gather | solution.py:383
  157.7 38.8 %all_gather.50 = bf16[384,768]{0,1:T(8,128)(2,1)S(1)} all-gather(bf16[384,48]{0,1:T(8,128)(2,1)S(1)} %copy-done.148), channel_id=1, replica_groups=mesh['dp'=16,'tensor'=2] {'dp'}, dimensions={1}, use_global_device_ids=true | all-gather | bytes 626688 | tf_op jit(solution)/shard_map/all_gather | solution.py:385
  199.9 2.3 collective-permute-done.1
  202.7 3.5 collective-permute-done.2
  207.4 3.6 collective-permute-done.3
  229.3 2.4 fusion
  260.4 10.4 %reduce-scatter.25.cloned.1.call-done = f32[256,768]{1,0:T(8,128)} async-done(((f32[512,768]{1,0:T(8,128)}), f32[256,768]{1,0:T(8,128)}) %reduce-scatter.25.cloned.1.call-update) | async-done | bytes 786448 | tf_op jit(solution)/shard_map/reduce_scatter | solution.py:241
  270.8 3.7 fusion.198
  276.3 2.8 all_gather.59
  279.1 42.1 %all-gather.7.cloned.1.call-done = bf16[768,1536]{1,0:T(8,128)(2,1)} async-done(((bf16[48,1536]{1,0:T(8,128)(2,1)}), bf16[768,1536]{1,0:T(8,128)(2,1)}) %all-gather.7.cloned.1.call-update) | async-done | bytes 2359312 | tf_op jit(solution)/shard_map/all_gather | solution.py:386
  321.2 10.4 %fusion.11 = (f32[512,1536]{1,0:T(8,128)}, f32[512,1536]{1,0:T(8,128)}) fusion(f32[1536]{0:T(1024)S(1)} %copy-done.207, bf16[512,768]{1,0:T(8,128)(2,1)S(1)} %all_gather.59, bf16[768,1536]{1,0:T(8,128)(2,1)} %all-gather.7.cloned.1.call-done), kind=kOutput, calls=%fused_computation.39 | convolution fusion | flops 1257504768 | bytes 9443328 | tf_op jit(solution)/shard_map/dot_general | solution.py:250
  331.7 52.7 %all-gather.9.cloned.1.call-done = bf16[1536,768]{0,1:T(8,128)(2,1)} async-done(((bf16[1536,48]{0,1:T(8,128)(2,1)}), bf16[1536,768]{0,1:T(8,128)(2,1)}) %all-gather.9.cloned.1.call-update) | async-done | bytes 2359312 | tf_op jit(solution)/shard_map/all_gather | solution.py:387
  384.4 6.1 fusion.35
  390.5 2.4 all_gather.57
  392.9 9.7 %fusion.10 = (f32[512,1536]{1,0:T(8,128)S(1)}, f32[512,1536]{1,0:T(8,128)S(1)}) fusion(f32[1536]{0:T(1024)} %param.28, bf16[512,768]{1,0:T(8,128)(2,1)S(1)} %all_gather.57, bf16[768,1536]{1,0:T(8,128)(2,1)} %all-gather.7.cloned.1.call-done), kind=kOutput, calls=%fused_computation.38 | convolution fusion | flops 1257504768 | bytes 9443328 | tf_op jit(solution)/shard_map/dot_general | solution.py:250
  405.2 2.6 fusion.34
  407.9 2.4 all_gather.55
  410.2 9.5 %fusion.9 = (f32[512,1536]{1,0:T(8,128)S(1)}, f32[512,1536]{1,0:T(8,128)S(1)}) fusion(f32[1536]{0:T(1024)} %param.28, bf16[512,768]{1,0:T(8,128)(2,1)S(1)} %all_gather.55, bf16[768,1536]{1,0:T(8,128)(2,1)} %all-gather.7.cloned.1.call-done), kind=kOutput, calls=%fused_computation.37 | convolution fusion | flops 1257504768 | bytes 9443328 | tf_op jit(solution)/shard_map/dot_general | solution.py:250
  422.5 2.6 fusion.33
  426.8 5.9 reduce-scatter.23.cloned.1.call-done
  432.8 4.5 fusion.197
  437.3 2.4 all_gather.51
  439.6 8.1 %fusion.8 = (f32[512,1536]{1,0:T(8,128)S(1)}, f32[512,1536]{1,0:T(8,128)S(1)}) fusion(f32[1536]{0:T(1024)S(1)} %copy-done.208, bf16[512,768]{1,0:T(8,128)(2,1)S(1)} %all_gather.51, bf16[768,1536]{1,0:T(8,128)(2,1)S(1)} %copy-done.206), kind=kOutput, calls=%fused_computation.36 | convolution fusion | flops 1257504768 | bytes 9443328 | tf_op jit(solution)/shard_map/dot_general | solution.py:250
  450.4 2.6 fusion.32
  453.2 10.4 %reduce-scatter.19.cloned.1.call-done = f32[256,768]{1,0:T(8,128)} async-done(((f32[512,768]{1,0:T(8,128)}), f32[256,768]{1,0:T(8,128)}) %reduce-scatter.19.cloned.1.call-update) | async-done | bytes 786448 | tf_op jit(solution)/shard_map/reduce_scatter | solution.py:260
  465.4 3.4 fusion.79
  471.1 2.5 all_gather.67
  473.6 7.8 fusion.43
  483.6 4.3 fusion.191
  488.9 2.5 all_gather.65
  491.4 7.8 fusion.42
  500.6 2.9 all_gather.60
  503.5 8.3 %fusion.40 = f32[512,768]{1,0:T(8,128)} fusion(bf16[768,1536]{1,0:T(8,128)(2,1)} %all-gather.7.cloned.1.call-done, f32[512,1536]{1,0:T(8,128)} %copy-done.86, f32[512,1536]{1,0:T(8,128)} %copy-done.87, bf16[512,768]{1,0:T(8,128)(2,1)} %all_gather.60, bf16[1536,768]{0,1:T(8,128)(2,1)S(1)} %copy-done.4), kind=kOutput, calls=%fused_computation.114 | convolution fusion | flops 2426929152 | bytes 13369344 | tf_op jit(solution)/shard_map/dot_general | solution.py:118
  513.2 2.5 all_gather.63
  515.7 7.8 fusion.41
  525.1 43.4 %all_gather.62 = bf16[2,768,8]{2,0,1:T(2,128)(2,1)S(1)} all-gather(bf16[2,48,8]{2,0,1:T(2,128)(2,1)} %copy.63), channel_id=1, replica_groups=mesh['dp'=16,'tensor'=2] {'dp'}, dimensions={1}, use_global_device_ids=true | all-gather | bytes 26112 | tf_op jit(solution)/shard_map/all_gather | solution.py:396
  573.4 2.6 pad_maximum_fusion.1
  576.1 3.1 multiply_reduce_fusion.7
  579.3 2.5 fusion.189
  582.0 2.5 all_gather.61
  585.2 4.6 convolution_convert_fusion.6
  592.8 2.5 all_gather.64
  600.4 2.4 all_gather.66
  609.0 2.5 all_gather.136
  617.3 4.7 multiply_reduce_fusion.3
  621.9 6.5 multiply_convert_fusion.3
  631.7 4.8 multiply_reduce_fusion.2
  636.5 4.7 multiply_reduce_fusion.1
  641.2 5.6 multiply_reduce_fusion
  648.3 2.1 add_convert_fusion.7
  650.5 7.1 multiply_convert_fusion.2
  659.4 4.9 multiply_convert_fusion.1
  666.1 4.7 multiply_convert_fusion
  679.0 2.2 convolution_bitcast_fusion.6
  705.2 71.8 %psum.34 = f32[2,8,384]{2,1,0:T(8,128)} all-reduce(f32[2,8,384]{2,1,0:T(8,128)S(1)} %fusion.110), channel_id=1, replica_groups=mesh['dp'=16,'tensor'=2] {'dp'}, use_global_device_ids=true, to_apply=%region_60.61 | all-reduce | flops 6144 | bytes 49152 | tf_op jit(solution)/shard_map/psum | solution.py:409
  781.2 2.1 add_bitcast_fusion.1
  784.4 3.1 pad_maximum_fusion
  (676 shorter events, 157.7 us)
Async XLA Ops:
  8.0 252.4 %reduce-scatter.21.cloned.1.call-start = ((), (), s32[]{:S(2)}) async-start(), calls=%async_computation.20 | async-start | bytes 2359296 | tf_op jit(solution)/shard_map/reduce_scatter | solution.py:241
  8.0 190.5 %collective-permute-start = (bf16[1,2,48,8]{2,3,1,0:T(8,128)(2,1)}, bf16[1,2,48,8]{2,3,1,0:T(8,128)(2,1)S(1)}, u32[]{:S(2)}, u32[]{:S(2)}) collective-permute-start(bf16[1,2,48,8]{2,3,1,0:T(8,128)(2,1)} %bitcast.523), channel_id=1, source_target_pairs={{0,2},{2,0},{4,6},{6,4},{8,10},{10,8},{12,14},{14,12},{16,18},{18,... | collective-permute-start | bytes 4616 | tf_op jit(solution)/shard_map/ppermute | solution.py:31
  55.6 58.8 %copy-start.19 = (bf16[768,384]{1,0:T(8,128)(2,1)}, bf16[768,384]{1,0:T(8,128)(2,1)S(1)}, u32[]{:S(2)}) copy-start(bf16[768,384]{1,0:T(8,128)(2,1)S(1)} %all_gather.48) | copy-start | bytes 1769476
  94.5 18.6 %copy-start.14 = (bf16[768,384]{1,0:T(8,128)(2,1)}, bf16[768,384]{1,0:T(8,128)(2,1)S(1)}, u32[]{:S(2)}) copy-start(bf16[768,384]{1,0:T(8,128)(2,1)S(1)} %all_gather.49) | copy-start | bytes 1769476
  101.4 139.6 %copy-start.90 = (bf16[512,384]{0,1:T(8,128)(2,1)}, bf16[512,384]{0,1:T(8,128)(2,1)S(1)}, u32[]{:S(2)}) copy-start(bf16[512,384]{0,1:T(8,128)(2,1)S(1)} %convolution_convert_fusion.9) | copy-start | bytes 1179652
  110.6 47.0 %copy-start.148 = (bf16[384,48]{0,1:T(8,128)(2,1)S(1)}, bf16[384,48]{0,1:T(8,128)(2,1)}, u32[]{:S(2)}) copy-start(bf16[384,48]{0,1:T(8,128)(2,1)} %param.26) | copy-start | bytes 110596
  113.1 84.8 %copy-start.81 = (bf16[1,512,768]{2,1,0:T(8,128)(2,1)}, bf16[1,512,768]{2,1,0:T(8,128)(2,1)S(1)}, u32[]{:S(2)}) copy-start(bf16[1,512,768]{2,1,0:T(8,128)(2,1)S(1)} %all-gather.1) | copy-start | bytes 2359300
  114.4 83.5 %copy-start.199 = (s32[4,1]{0,1:T(1,128)S(1)}, s32[4,1]{0,1:T(1,128)}, u32[]{:S(2)}) copy-start(s32[4,1]{0,1:T(1,128)} %param.19) | copy-start | bytes 52
  114.4 84.1 %copy-start.162 = (bf16[2,48,8]{1,2,0:T(8,128)(2,1)S(1)}, bf16[2,48,8]{1,2,0:T(8,128)(2,1)}, u32[]{:S(2)}) copy-start(bf16[2,48,8]{1,2,0:T(8,128)(2,1)} %param.24) | copy-start | bytes 4612
  115.8 96.9 %copy-start.105 = (bf16[2,8,384]{2,1,0:T(8,128)(2,1)S(1)}, bf16[2,8,384]{2,1,0:T(8,128)(2,1)}, u32[]{:S(2)}) copy-start(bf16[2,8,384]{2,1,0:T(8,128)(2,1)} %param.25) | copy-start | bytes 36868
  157.7 91.3 %copy-start.22 = (bf16[768,384]{1,0:T(8,128)(2,1)}, bf16[768,384]{1,0:T(8,128)(2,1)S(1)}, u32[]{:S(2)}) copy-start(bf16[768,384]{1,0:T(8,128)(2,1)S(1)} %all_gather.47) | copy-start | bytes 1769476
  196.5 59.6 %copy-start.24 = (bf16[384,768]{0,1:T(8,128)(2,1)}, bf16[384,768]{0,1:T(8,128)(2,1)S(1)}, u32[]{:S(2)}) copy-start(bf16[384,768]{0,1:T(8,128)(2,1)S(1)} %all_gather.50) | copy-start | bytes 1769476
  198.6 3.7 collective-permute-start.1
  202.3 3.8 collective-permute-start.2
  202.7 16.2 %copy-start.41 = (pred[512,512]{0,1:T(8,128)(4,1)}, pred[512,512]{0,1:T(8,128)(4,1)S(1)}, u32[]{:S(2)}) copy-start(pred[512,512]{0,1:T(8,128)(4,1)S(1)} %compare_and_fusion.2) | copy-start | bytes 786436
  206.2 4.9 collective-permute-start.3
  223.7 36.7 %reduce-scatter.17.cloned.1.call-start = ((), (), s32[]{:S(2)}) async-start(), calls=%async_computation.16 | async-start | bytes 2359296 | tf_op jit(solution)/shard_map/reduce_scatter | solution.py:241
  238.0 22.4 %reduce-scatter.29.cloned.1.call-start = ((), (), s32[]{:S(2)}) async-start(), calls=%async_computation.24 | async-start | bytes 2359296 | tf_op jit(solution)/shard_map/reduce_scatter | solution.py:241
  248.4 22.4 %reduce-scatter.25.cloned.1.call-start = ((), (), s32[]{:S(2)}) async-start(), calls=%async_computation.22 | async-start | bytes 2359296 | tf_op jit(solution)/shard_map/reduce_scatter | solution.py:241
  256.1 14.7 %copy-start.53 = (bf16[4,256,768]{2,1,0:T(8,128)(2,1)S(1)}, bf16[4,256,768]{2,1,0:T(8,128)(2,1)}, u32[]{:S(2)}) copy-start(bf16[4,256,768]{2,1,0:T(8,128)(2,1)} %param.17) | copy-start | bytes 4718596
  257.9 63.3 %all-gather.7.cloned.1.call-start = ((), (), s32[]{:S(2)}) async-start(), calls=%async_computation.17 | async-start | bytes 2506752 | tf_op jit(solution)/shard_map/all_gather | solution.py:386
  258.5 125.9 %all-gather.9.cloned.1.call-start = ((), (), s32[]{:S(2)}) async-start(), calls=%async_computation.18 | async-start | bytes 2506752 | tf_op jit(solution)/shard_map/all_gather | solution.py:387
  259.1 167.7 %reduce-scatter.31.cloned.1.call-start = ((), (), s32[]{:S(2)}) async-start(), calls=%async_computation.25 | async-start | bytes 2359296 | tf_op jit(solution)/shard_map/reduce_scatter | solution.py:260
  274.8 46.4 %copy-start.207 = (f32[1536]{0:T(1024)S(1)}, f32[1536]{0:T(1024)}, u32[]{:S(2)}) copy-start(f32[1536]{0:T(1024)} %param.28) | copy-start | bytes 18436
  390.5 36.3 %reduce-scatter.27.cloned.1.call-start = ((), (), s32[]{:S(2)}) async-start(), calls=%async_computation.23 | async-start | bytes 2359296 | tf_op jit(solution)/shard_map/reduce_scatter | solution.py:260
  392.9 12.4 %copy-start.4 = (bf16[1536,768]{0,1:T(8,128)(2,1)S(1)}, bf16[1536,768]{0,1:T(8,128)(2,1)}, u32[]{:S(2)}) copy-start(bf16[1536,768]{0,1:T(8,128)(2,1)} %all-gather.9.cloned.1.call-done) | copy-start | bytes 7077892
  407.8 24.9 %reduce-scatter.23.cloned.1.call-start = ((), (), s32[]{:S(2)}) async-start(), calls=%async_computation.21 | async-start | bytes 2359296 | tf_op jit(solution)/shard_map/reduce_scatter | solution.py:260
  422.5 10.2 %copy-start.146 = (f32[768]{0:T(1024)S(1)}, f32[768]{0:T(1024)}, u32[]{:S(2)}) copy-start(f32[768]{0:T(1024)} %get-tuple-element.175) | copy-start | bytes 9220
  422.5 10.2 %copy-start.150 = (f32[256]{0:T(256)S(1)}, f32[256]{0:T(256)}, u32[]{:S(2)}) copy-start(f32[256]{0:T(256)} %copy-done.149) | copy-start | bytes 3076
  422.5 10.2 %copy-start.154 = (f32[256]{0:T(256)S(1)}, f32[256]{0:T(256)}, u32[]{:S(2)}) copy-start(f32[256]{0:T(256)} %copy-done.153) | copy-start | bytes 3076
  422.5 10.2 %copy-start.158 = (f32[256]{0:T(256)S(1)}, f32[256]{0:T(256)}, u32[]{:S(2)}) copy-start(f32[256]{0:T(256)} %copy-done.157) | copy-start | bytes 3076
  422.5 10.2 %copy-start.172 = (f32[256]{0:T(256)S(1)}, f32[256]{0:T(256)}, u32[]{:S(2)}) copy-start(f32[256]{0:T(256)} %copy-done.171) | copy-start | bytes 3076
  422.5 10.2 %copy-start.175 = (f32[256]{0:T(256)S(1)}, f32[256]{0:T(256)}, u32[]{:S(2)}) copy-start(f32[256]{0:T(256)} %copy-done.174) | copy-start | bytes 3076
  422.5 10.2 %copy-start.178 = (f32[256]{0:T(256)S(1)}, f32[256]{0:T(256)}, u32[]{:S(2)}) copy-start(f32[256]{0:T(256)} %copy-done.177) | copy-start | bytes 3076
  425.1 38.4 %reduce-scatter.19.cloned.1.call-start = ((), (), s32[]{:S(2)}) async-start(), calls=%async_computation.19 | async-start | bytes 2359296 | tf_op jit(solution)/shard_map/reduce_scatter | solution.py:260
  426.7 10.5 %copy-start.196 = (f32[256]{0:T(256)}, f32[256]{0:T(256)S(1)}, u32[]{:S(2)}) copy-start(f32[256]{0:T(256)S(1)} %multiply_reduce_fusion.15) | copy-start | bytes 3076
  426.8 36.8 %copy-start.160 = (f32[256]{0:T(256)}, f32[256]{0:T(256)S(1)}, u32[]{:S(2)}) copy-start(f32[256]{0:T(256)S(1)} %fusion.157) | copy-start | bytes 3076
  453.0 122.9 %reduce-scatter.45.cloned.1.call-start = ((), (), s32[]{:S(2)}) async-start(), calls=%async_computation.32 | async-start | bytes 2359296 | tf_op jit(solution)/shard_map/reduce_scatter | solution.py:302
  453.1 15.8 %copy-start.186 = (f32[256]{0:T(256)}, f32[256]{0:T(256)S(1)}, u32[]{:S(2)}) copy-start(f32[256]{0:T(256)S(1)} %broadcast_multiply_fusion.4) | copy-start | bytes 3076
  453.1 15.8 %copy-start.187 = (f32[256]{0:T(256)}, f32[256]{0:T(256)S(1)}, u32[]{:S(2)}) copy-start(f32[256]{0:T(256)S(1)} %broadcast_multiply_fusion.2) | copy-start | bytes 3076
  453.1 15.8 %copy-start.189 = (f32[256]{0:T(256)}, f32[256]{0:T(256)S(1)}, u32[]{:S(2)}) copy-start(f32[256]{0:T(256)S(1)} %broadcast_multiply_fusion) | copy-start | bytes 3076
  473.6 10.0 %copy-start.145 = (f32[768]{0:T(1024)S(1)}, f32[768]{0:T(1024)}, u32[]{:S(2)}) copy-start(f32[768]{0:T(1024)} %get-tuple-element.173) | copy-start | bytes 9220
  481.4 94.6 %reduce-scatter.41.cloned.1.call-start = ((), (), s32[]{:S(2)}) async-start(), calls=%async_computation.30 | async-start | bytes 2359296 | tf_op jit(solution)/shard_map/reduce_scatter | solution.py:302
  487.9 11.3 %copy-start.165 = (f32[256]{0:T(256)}, f32[256]{0:T(256)S(1)}, u32[]{:S(2)}) copy-start(f32[256]{0:T(256)S(1)} %negate_multiply_fusion.7) | copy-start | bytes 3076
  499.3 76.8 %reduce-scatter.33.cloned.1.call-start = ((), (), s32[]{:S(2)}) async-start(), calls=%async_computation.26 | async-start | bytes 2359296 | tf_op jit(solution)/shard_map/reduce_scatter | solution.py:302
  499.3 12.5 %copy-start.169 = (f32[256]{0:T(256)}, f32[256]{0:T(256)S(1)}, u32[]{:S(2)}) copy-start(f32[256]{0:T(256)S(1)} %negate_multiply_fusion.11) | copy-start | bytes 3076
  511.8 67.4 %reduce-scatter.37.cloned.1.call-start = ((), (), s32[]{:S(2)}) async-start(), calls=%async_computation.28 | async-start | bytes 2359296 | tf_op jit(solution)/shard_map/reduce_scatter | solution.py:302
  511.9 11.6 %copy-start.167 = (f32[256]{0:T(256)}, f32[256]{0:T(256)S(1)}, u32[]{:S(2)}) copy-start(f32[256]{0:T(256)S(1)} %negate_multiply_fusion.9) | copy-start | bytes 3076
  523.5 52.6 %copy-start.5 = (f32[256,768]{1,0:T(8,128)S(1)}, f32[256,768]{1,0:T(8,128)}, u32[]{:S(2)}) copy-start(f32[256,768]{1,0:T(8,128)} %get-tuple-element.269) | copy-start | bytes 2359300
  523.5 52.6 %copy-start.7 = (f32[256,768]{1,0:T(8,128)S(1)}, f32[256,768]{1,0:T(8,128)}, u32[]{:S(2)}) copy-start(f32[256,768]{1,0:T(8,128)} %copy-done.6) | copy-start | bytes 2359300
  523.5 52.6 %copy-start.9 = (f32[256,768]{1,0:T(8,128)S(1)}, f32[256,768]{1,0:T(8,128)}, u32[]{:S(2)}) copy-start(f32[256,768]{1,0:T(8,128)} %copy-done.8) | copy-start | bytes 2359300
  523.5 52.6 %copy-start.151 = (f32[256]{0:T(256)S(1)}, f32[256]{0:T(256)}, u32[]{:S(2)}) copy-start(f32[256]{0:T(256)} %copy-done.149) | copy-start | bytes 3076
  523.5 52.6 %copy-start.155 = (f32[256]{0:T(256)S(1)}, f32[256]{0:T(256)}, u32[]{:S(2)}) copy-start(f32[256]{0:T(256)} %copy-done.153) | copy-start | bytes 3076
  523.5 253.5 %reduce-scatter.35.cloned.1.call-start = ((), (), s32[]{:S(2)}) async-start(), calls=%async_computation.27 | async-start | bytes 1179648 | tf_op jit(solution)/shard_map/reduce_scatter | solution.py:330
  585.2 10.7 %slice-start = ((s8[6291456]{0:T(1024)(128)(4,1)}), s8[4194304]{0:T(1024)(128)(4,1)S(1)}, s32[]{:S(2)}) async-start(s8[6291456]{0:T(1024)(128)(4,1)} %bitcast.439), calls=%async_computation.34 | async-start | bytes 8388608
  650.5 128.6 %reduce-scatter.39.cloned.1.call-start = ((), (), s32[]{:S(2)}) async-start(), calls=%async_computation.29 | async-start | bytes 1179648 | tf_op jit(solution)/shard_map/reduce_scatter | solution.py:330
  678.7 102.4 %reduce-scatter.43.cloned.1.call-start = ((), (), s32[]{:S(2)}) async-start(), calls=%async_computation.31 | async-start | bytes 1179648 | tf_op jit(solution)/shard_map/reduce_scatter | solution.py:330
  688.5 94.7 %reduce-scatter.47.cloned.1.call-start = ((), (), s32[]{:S(2)}) async-start(), calls=%async_computation.33 | async-start | bytes 1179648 | tf_op jit(solution)/shard_map/reduce_scatter | solution.py:330
  695.9 81.1 %copy-start.181 = (f32[256]{0:T(256)S(1)}, f32[256]{0:T(256)}, u32[]{:S(2)}) copy-start(f32[256]{0:T(256)} %copy-done.180) | copy-start | bytes 3076
  697.9 79.1 %copy-start.33 = (f32[256,768]{1,0:T(8,128)S(1)}, f32[256,768]{1,0:T(8,128)}, u32[]{:S(2)}) copy-start(f32[256,768]{1,0:T(8,128)} %copy-done.32) | copy-start | bytes 2359300
  697.9 81.1 %copy-start.37 = (f32[256,768]{1,0:T(8,128)S(1)}, f32[256,768]{1,0:T(8,128)}, u32[]{:S(2)}) copy-start(f32[256,768]{1,0:T(8,128)} %copy-done.36) | copy-start | bytes 2359300
  698.0 83.2 %copy-start.35 = (f32[256,768]{1,0:T(8,128)S(1)}, f32[256,768]{1,0:T(8,128)}, u32[]{:S(2)}) copy-start(f32[256,768]{1,0:T(8,128)} %copy-done.34) | copy-start | bytes 2359300
  703.0 80.3 %copy-start.40 = (f32[256,768]{1,0:T(8,128)S(1)}, f32[256,768]{1,0:T(8,128)}, u32[]{:S(2)}) copy-start(f32[256,768]{1,0:T(8,128)} %copy-done.39) | copy-start | bytes 2359300
  703.0 80.3 %copy-start.185 = (f32[256]{0:T(256)S(1)}, f32[256]{0:T(256)}, u32[]{:S(2)}) copy-start(f32[256]{0:T(256)} %copy-done.184) | copy-start | bytes 3076
  (181 other events, 678.3 us)
Sparse Core Ops, SparseCore 0:
  223.8 7.2 reduce-scatter.20
  238.1 7.0 reduce-scatter.16
  248.5 9.1 reduce-scatter.28
  260.4 10.3 reduce-scatter.24
  390.6 7.4 reduce-scatter.30
  407.9 7.4 reduce-scatter.26
  425.2 7.4 reduce-scatter.22
  453.2 10.3 reduce-scatter.18
  481.6 10.3 reduce-scatter.44
  499.4 10.3 reduce-scatter.40
  512.6 10.3 reduce-scatter.32
  525.0 10.3 reduce-scatter.36
  650.6 4.0 reduce-scatter.34
  678.8 4.0 reduce-scatter.38
  688.6 5.7 reduce-scatter.42
  698.1 8.2 reduce-scatter.46
Sparse Core Ops, SparseCore 1:
  261.2 60.0 all-gather.6
  323.9 60.4 all-gather.8
